TPU v7x, 32 devices: a whole 2x2x4 slice. The times are simulated.
32 devices in a mesh: row: 2 (over core), col: 16 (over z, y, x).
Axes of the slice: x: 2, y: 2, z: 4, core: 2. Of those that a mesh axis runs over, the one named last changes fastest.
Arguments:
- object_in: float32 [2, 2, 512, 4096], P(None, None, 'row', 'col'), may hold values from -4 to 4
- probe_in: float32 [2, 256, 256], replicated, may hold values from -5 to 5
- positions: int32 [2, 16, 2, 2], P('row', 'col'), may hold values from -32 to 32
- intensity: float32 [2, 16, 2, 256, 256], P('row', 'col'), may hold values from 0.1 to 8.2
Outputs:
- object_out: float32 [2, 2, 512, 4096], P(None, None, 'row', 'col')
- probe_out: float32 [2, 256, 256], replicated
Inputs may be any that keep to these rules, and one draw needn't show every extreme that they name: positions[r, c, p] = (dy, dx) places the probe of position p on object rows r * 256 + dy to r * 256 + dy + 255 and columns c * 256 + dx to c * 256 + dx + 255.
All inputs are finite; a program needn't handle non-finite values.
Results may differ from a plain program's by a relative error of at most 0.0003.
Values sent between devices are 32-bit elements; how exact they have to be, the bound alone decides.
No kernel may reach another device: no remote copies, remote signals or barrier semaphores. Data moves between devices by JAX's collectives and lax.ppermute only.
A program may use at most 64 MiB of HBM per device.

v0:
```python
import math
import jax
import jax.numpy as jnp
from jax import lax
from jax.sharding import PartitionSpec as P

RIM = 32


def passed_along(value, axis, steps):
    count = lax.axis_size(axis)
    initial, last = (max(0, -steps), min(count, count - steps))
    return lax.ppermute(value, axis, [(source, source + steps) for source in range(initial, last)])


def extended(cells, sides, width):
    for axis, dim in sides:
        count = lax.axis_size(axis)
        ends = count - 1
        head = lax.slice_in_dim(cells, 0, width, axis=dim)
        tail = lax.slice_in_dim(cells, cells.shape[dim] - width, cells.shape[dim], axis=dim)
        cells = jnp.concatenate(
            [
                lax.ppermute(tail, axis, [(i, (i + 1) % count) for i in range(ends)]),
                cells,
                lax.ppermute(head, axis, [((i + 1) % count, i) for i in range(ends)]),
            ],
            axis=dim,
        )
    return cells


def tables(extent):
    line_idx = jnp.arange(extent, dtype=jnp.int32)
    turn_count = line_idx[:, None] * line_idx[None, :] % extent
    angles = turn_count.astype(jnp.float32) * (2.0 * math.pi / extent)
    factor = 1.0 / math.sqrt(extent)
    cosine = jnp.cos(angles) * factor
    sine_tab = jnp.sin(angles) * factor
    frequency = ((line_idx + extent // 2) % extent - extent // 2).astype(jnp.float32)
    phases = (
        -math.pi * 8.0 / (extent * extent) * (frequency[:, None] ** 2 + frequency[None, :] ** 2)
    )
    return (cosine, sine_tab, jnp.cos(phases), jnp.sin(phases))


def matrices(cosine, sine_tab, orient):
    return (cosine, sine_tab, float(orient))


def transform(real_part, imag_part, tables_pair):
    cosine, sine_tab, orient = tables_pair
    high = lax.Precision.HIGHEST
    rc = jnp.einsum("byx,xk->byk", real_part, cosine, precision=high)
    rs = jnp.einsum("byx,xk->byk", real_part, sine_tab, precision=high)
    ic = jnp.einsum("byx,xk->byk", imag_part, cosine, precision=high)
    isn = jnp.einsum("byx,xk->byk", imag_part, sine_tab, precision=high)
    mid_re = rc + orient * isn
    mid_im = ic - orient * rs
    out_re = jnp.einsum("ky,byx->bkx", cosine, mid_re, precision=high) + orient * jnp.einsum(
        "ky,byx->bkx", sine_tab, mid_im, precision=high
    )
    out_im = jnp.einsum("ky,byx->bkx", cosine, mid_im, precision=high) - orient * jnp.einsum(
        "ky,byx->bkx", sine_tab, mid_re, precision=high
    )
    return (out_re, out_im)


def times_plain(first_re, first_im, second_re, second_im):
    return (
        first_re * second_re - first_im * second_im,
        first_re * second_im + first_im * second_re,
    )


def times_conj(first_re, first_im, second_re, second_im):
    return (
        first_re * second_re + first_im * second_im,
        first_re * second_im - first_im * second_re,
    )


def tile_gradient(window, probe, offsets, measured, constants):
    cosine, sine_tab, kern_re, kern_im = constants
    forward = matrices(cosine, sine_tab, 1)
    backward = matrices(cosine, sine_tab, -1)
    extent = probe.shape[-1]
    zero_idx = jnp.zeros((), jnp.int32)

    def cut_patch(offset):
        return lax.dynamic_slice(
            window, (zero_idx, zero_idx, offset[0] + RIM, offset[1] + RIM), (2, 2, extent, extent)
        )

    patches = jax.vmap(cut_patch)(offsets)
    first_re, first_im = (patches[:, 0, 0], patches[:, 0, 1])
    second_re, second_im = (patches[:, 1, 0], patches[:, 1, 1])
    probe_re, probe_im = (probe[0], probe[1])
    wave_re, wave_im = times_plain(probe_re, probe_im, first_re, first_im)
    spec_re, spec_im = transform(wave_re, wave_im, forward)
    spec_re, spec_im = times_plain(kern_re, kern_im, spec_re, spec_im)
    prop_re, prop_im = transform(spec_re, spec_im, backward)
    exit_re, exit_im = times_plain(prop_re, prop_im, second_re, second_im)
    far_re, far_im = transform(exit_re, exit_im, forward)
    excess = 2.0 * (far_re * far_re + far_im * far_im - measured)
    back_re, back_im = transform(excess * far_re, excess * far_im, backward)
    grad2_re, grad2_im = times_conj(prop_re, prop_im, back_re, back_im)
    lift_re, lift_im = times_conj(second_re, second_im, back_re, back_im)
    lift_re, lift_im = transform(lift_re, lift_im, forward)
    lift_re, lift_im = times_conj(kern_re, kern_im, lift_re, lift_im)
    enter_re, enter_im = transform(lift_re, lift_im, backward)
    grad1_re, grad1_im = times_conj(probe_re, probe_im, enter_re, enter_im)
    probe_re_g, probe_im_g = times_conj(first_re, first_im, enter_re, enter_im)
    probe_grad = jnp.stack([jnp.sum(probe_re_g, 0), jnp.sum(probe_im_g, 0)], 0)
    pieces = jnp.stack([jnp.stack([grad1_re, grad1_im], 1), jnp.stack([grad2_re, grad2_im], 1)], 1)
    gradient = jnp.zeros(window.shape, jnp.float32)
    for position in range(offsets.shape[0]):
        start_at = (zero_idx, zero_idx, offsets[position, 0] + RIM, offsets[position, 1] + RIM)
        current = lax.dynamic_slice(gradient, start_at, pieces.shape[1:])
        gradient = lax.dynamic_update_slice(gradient, current + pieces[position], start_at)
    return (gradient, probe_grad)


def turned(block):
    return jnp.swapaxes(block, 2, 3)


def rows_then_cols(gradient):
    inner_px = gradient.shape[-1] - 2 * RIM
    upper_end = RIM + inner_px
    from_below = passed_along(gradient[:, :, :RIM, :], "row", -1)
    from_above = passed_along(gradient[:, :, upper_end:, :], "row", 1)
    middle = gradient[:, :, RIM:upper_end, :]
    middle = middle.at[:, :, inner_px - RIM :, :].add(from_below)
    middle = middle.at[:, :, :RIM, :].add(from_above)
    from_right = turned(passed_along(turned(middle[..., :RIM]), "col", -1))
    from_left = turned(passed_along(turned(middle[..., upper_end:]), "col", 1))
    interior = middle[..., RIM:upper_end]
    interior = interior.at[..., inner_px - RIM :].add(from_right)
    interior = interior.at[..., :RIM].add(from_left)
    return interior


def local(object_in, probe_in, positions, intensity):
    extent = probe_in.shape[-1]
    constants = tables(extent)
    offsets = positions.reshape(-1, 2)
    measured = intensity.reshape(-1, extent, extent)
    tile_total = lax.axis_size("row") * lax.axis_size("col")
    probe_rate = 2.0 / tile_total
    current = object_in
    window = extended(current, (("row", 2), ("col", 3)), RIM)
    gradient, probe_grad = tile_gradient(window, probe_in, offsets, measured, constants)
    probe_total = lax.psum(probe_grad, ("row", "col"))
    probe_next = probe_in - probe_rate * probe_total
    descent = rows_then_cols(gradient)
    local_peak = jnp.max(descent[:, 0] ** 2 + descent[:, 1] ** 2)
    largest = lax.pmax(local_peak, ("row", "col"))
    current = current - 0.3 * descent / (jnp.sqrt(largest) + 1e-06)
    return (current, probe_next)


def solution(mesh):
    placed = (
        P(None, None, "row", "col"),
        P(),
        P("row", "col", None, None),
        P("row", "col", None, None, None),
    )
    return jax.shard_map(
        local,
        mesh=mesh,
        in_specs=placed,
        out_specs=(P(None, None, "row", "col"), P()),
        check_vma=False,
    )
```

profile of v0, /device:TPU:0, one launch (start us, length us, event | category | flops | bytes accessed | tf_op | source)
XLA Modules:
  0.0 372.2 jit_solution(18278796465916017940)
XLA Ops:
  10.1 2.4 collective-permute-start
  22.2 2.0 copy.98
  24.5 4.2 %collective-permute-start.2 = (f32[2,2,320,32]{2,3,1,0:T(8,128)S(1)}, f32[2,2,320,32]{2,3,1,0:T(8,128)S(1)}, u32[]{:S(2)}, u32[]{:S(2)}) collective-permute-start(f32[2,2,320,32]{2,3,1,0:T(8,128)S(1)} %get-tuple-element.84), channel_id=1, source_target_pairs={{0,1},{1,2},{2,3},{3,4},{4,5},{5,6},{6,7},{7,8},{8,9},{9,10},{10,1... | collective-permute-start | bytes 491528 | tf_op jit(solution)/shard_map/ppermute | solution.py:24
  30.1 3.7 collective-permute-done.2
  33.8 6.2 %collective-permute-done.3 = f32[2,2,320,32]{2,3,1,0:T(8,128)S(1)} collective-permute-done((f32[2,2,320,32]{2,3,1,0:T(8,128)S(1)}, f32[2,2,320,32]{2,3,1,0:T(8,128)S(1)}, u32[]{:S(2)}, u32[]{:S(2)}) %collective-permute-start.3) | collective-permute-done | bytes 163872 | tf_op jit(solution)/shard_map/ppermute | solution.py:26
  41.8 11.3 %while.5 = (s32[]{:T(128)}, f32[2,2,320,320]{2,3,1,0:T(8,128)S(1)}, s32[2,4]{1,0:T(2,128)S(1)}, f32[2,2,2,256,256]{3,4,0,2,1:T(8,128)}, s32[]{:T(128)}) while((s32[]{:T(128)}, f32[2,2,320,320]{2,3,1,0:T(8,128)S(1)}, s32[2,4]{1,0:T(2,128)S(1)}, f32[2,2,2,256,256]{3,4,0,2,1:T(8,128)}, s32[]{:T(128)}) %tuple.62), condition=%wide.while_cond.4, body=%wide.while_body.4.sunk | while | flops 2 | bytes 21496496 | solution.py:91
  53.1 3.4 fusion.112
  56.5 3.2 fusion.116
  67.2 2.3 fusion.22
  78.8 2.1 fusion.20
  84.6 1.9 fusion.32
  90.1 2.0 convolution_add_fusion.3
  101.4 1.9 fusion.92
  103.3 2.3 fusion.88
  105.7 1.9 fusion.13
  107.6 1.9 fusion.12
  115.1 2.2 add_bitcast_fusion
  126.4 2.1 fusion.82
  136.0 1.9 fusion.5
  137.9 2.3 fusion.4
  145.6 2.8 fusion.38
  150.1 13.4 %dynamic_update_slice.6 = f32[2,2,320,320]{2,3,1,0:T(8,128)S(1)} dynamic-update-slice(f32[2,2,320,320]{2,3,1,0:T(8,128)S(1)} %broadcast_in_dim.2, f32[2,2,256,256]{2,3,1,0:T(8,128)} %fusion.25, s32[]{:T(128)} %constant.162.clone.1, s32[]{:T(128)} %constant.162.clone.1, s32[]{:T(128)S(6)} %select_n.155, s32[]{:T(128)S(6)} %select_n.156) | dynamic-update-slice | bytes 2097156 | tf_op jit(solution)/shard_map/dynamic_update_slice | solution.py:120
  163.5 2.4 fusion.27
  165.9 14.0 %dynamic_update_slice.7 = f32[2,2,320,320]{2,3,1,0:T(8,128)S(1)} dynamic-update-slice(f32[2,2,320,320]{2,3,1,0:T(8,128)S(1)} %dynamic_update_slice.6, f32[2,2,256,256]{2,3,1,0:T(8,128)} %fusion.27, s32[]{:T(128)} %constant.162.clone.1, s32[]{:T(128)} %constant.162.clone.1, s32[]{:T(128)S(6)} %select_n.157, s32[]{:T(128)S(6)} %select_n.158) | dynamic-update-slice | bytes 2097156 | tf_op jit(solution)/shard_map/dynamic_update_slice | solution.py:120
  181.8 2.0 copy.129
  187.1 4.4 %collective-permute-start.5 = (f32[2,2,32,320]{3,2,1,0:T(8,128)}, f32[2,2,32,320]{3,2,1,0:T(8,128)}, u32[]{:S(2)}, u32[]{:S(2)}) collective-permute-start(f32[2,2,32,320]{3,2,1,0:T(8,128)} %copy.126), channel_id=1, source_target_pairs={{0,16},{1,17},{2,18},{3,19},{4,20},{5,21},{6,22},{7,23},{8,24},{9,... | collective-permute-start | bytes 491528 | tf_op jit(solution)/shard_map/ppermute | solution.py:13
  192.8 3.7 %scatter-add.14 = f32[2,2,256,320]{2,3,1,0:T(8,128)} dynamic-update-slice(f32[2,2,256,320]{2,3,1,0:T(8,128)} %slice.249, f32[2,2,32,320]{2,3,1,0:T(8,128)S(1)} %slice_add_fusion.1, s32[]{:T(128)} %constant.162.clone.1, s32[]{:T(128)} %constant.162.clone.1, s32[]{:T(128)} %constant.175.clone.1, s32[]{:T(128)} %constant.162.clone.1) | dynamic-update-slice | bytes 327684 | tf_op jit(solution)/shard_map/scatter-add | solution.py:134
  198.8 3.6 scatter-add.15
  206.8 4.7 %collective-permute-start.7 = (f32[2,2,32,256]{3,2,1,0:T(8,128)S(1)}, f32[2,2,32,256]{3,2,1,0:T(8,128)S(1)}, u32[]{:S(2)}, u32[]{:S(2)}) collective-permute-start(f32[2,2,32,256]{3,2,1,0:T(8,128)S(1)} %get-tuple-element.90), channel_id=1, source_target_pairs={{0,1},{1,2},{2,3},{3,4},{4,5},{5,6},{6,7},{7,8},{8,9},{9,10},{10,1... | collective-permute-start | bytes 393224 | tf_op jit(solution)/shard_map/ppermute | solution.py:13
  211.5 105.9 %all-reduce.2.cloned.1.call-done = f32[2,256,256]{1,2,0:T(8,128)} async-done(((f32[2,256,256]{1,2,0:T(8,128)}), f32[2,256,256]{1,2,0:T(8,128)}) %all-reduce.2.cloned.1.call-update) | async-done | bytes 524304 | tf_op jit(solution)/shard_map/psum | solution.py:154
  321.3 39.5 %pmax.7 = f32[]{:T(128)} all-reduce(f32[]{:T(128)} %fusion.29), channel_id=1, replica_groups=mesh['row'=2,'col'=16] {'row','col'}, use_global_device_ids=true, to_apply=%region_1.2 | all-reduce | flops 1 | bytes 8 | tf_op jit(solution)/shard_map/pmax | solution.py:158
  362.6 2.5 copy.130
  (129 shorter events, 102.3 us)
Async XLA Ops:
  7.2 6.7 %copy-start.15 = (s32[1,1,2,2]{3,2,1,0:T(2,128)S(1)}, s32[1,1,2,2]{3,2,1,0:T(2,128)}, u32[]{:S(2)}) copy-start(s32[1,1,2,2]{3,2,1,0:T(2,128)} %param.14) | copy-start | bytes 52
  7.2 12.2 %copy-start.12 = (f32[2,256,256]{2,1,0:T(8,128)S(1)}, f32[2,256,256]{2,1,0:T(8,128)}, u32[]{:S(2)}) copy-start(f32[2,256,256]{2,1,0:T(8,128)} %param.13) | copy-start | bytes 1572868
  7.2 310.2 %all-reduce.2.cloned.1.call-start = ((), (), s32[]{:S(2)}) async-start(), calls=%async_computation | async-start | bytes 1048576 | tf_op jit(solution)/shard_map/psum | solution.py:154
  8.8 31.1 %copy-start.2 = (f32[2,2,256,256]{2,3,1,0:T(8,128)}, f32[2,2,256,256]{2,3,1,0:T(8,128)S(1)}, u32[]{:S(2)}) copy-start(f32[2,2,256,256]{2,3,1,0:T(8,128)S(1)} %copy.128) | copy-start | bytes 3145732
  10.1 14.2 %collective-permute-start = (f32[2,2,32,256]{2,3,1,0:T(8,128)}, f32[2,2,32,256]{2,3,1,0:T(8,128)S(1)}, u32[]{:S(2)}, u32[]{:S(2)}) collective-permute-start(f32[2,2,32,256]{2,3,1,0:T(8,128)} %get-tuple-element.96), channel_id=1, source_target_pairs={{0,16},{1,17},{2,18},{3,19},{4,20},{5,21},{6,22},{7,23},{8,24},{9,... | collective-permute-start | bytes 393224 | tf_op jit(solution)/shard_map/ppermute | solution.py:24
  12.5 11.7 %collective-permute-start.1 = (f32[2,2,32,256]{2,3,1,0:T(8,128)}, f32[2,2,32,256]{2,3,1,0:T(8,128)S(1)}, u32[]{:S(2)}, u32[]{:S(2)}) collective-permute-start(f32[2,2,32,256]{2,3,1,0:T(8,128)} %get-tuple-element.97), channel_id=1, source_target_pairs={{16,0},{17,1},{18,2},{19,3},{20,4},{21,5},{22,6},{23,7},{24,8},{25... | collective-permute-start | bytes 393224 | tf_op jit(solution)/shard_map/ppermute | solution.py:26
  24.3 9.5 %copy-start.9 = (f32[2,2,32,256]{2,3,1,0:T(8,128)}, f32[2,2,32,256]{2,3,1,0:T(8,128)S(1)}, u32[]{:S(2)}) copy-start(f32[2,2,32,256]{2,3,1,0:T(8,128)S(1)} %collective-permute-done) | copy-start | bytes 393220
  24.3 9.5 %copy-start.10 = (f32[2,2,32,256]{2,3,1,0:T(8,128)}, f32[2,2,32,256]{2,3,1,0:T(8,128)S(1)}, u32[]{:S(2)}) copy-start(f32[2,2,32,256]{2,3,1,0:T(8,128)S(1)} %collective-permute-done.1) | copy-start | bytes 393220
  24.5 9.3 %collective-permute-start.2 = (f32[2,2,320,32]{2,3,1,0:T(8,128)S(1)}, f32[2,2,320,32]{2,3,1,0:T(8,128)S(1)}, u32[]{:S(2)}, u32[]{:S(2)}) collective-permute-start(f32[2,2,320,32]{2,3,1,0:T(8,128)S(1)} %get-tuple-element.84), channel_id=1, source_target_pairs={{0,1},{1,2},{2,3},{3,4},{4,5},{5,6},{6,7},{7,8},{8,9},{9,10},{10,1... | collective-permute-start | bytes 491528 | tf_op jit(solution)/shard_map/ppermute | solution.py:24
  28.7 11.2 %collective-permute-start.3 = (f32[2,2,320,32]{2,3,1,0:T(8,128)S(1)}, f32[2,2,320,32]{2,3,1,0:T(8,128)S(1)}, u32[]{:S(2)}, u32[]{:S(2)}) collective-permute-start(f32[2,2,320,32]{2,3,1,0:T(8,128)S(1)} %get-tuple-element.85), channel_id=1, source_target_pairs={{1,0},{2,1},{3,2},{4,3},{5,4},{6,5},{7,6},{8,7},{9,8},{10,9},{11,1... | collective-permute-start | bytes 491528 | tf_op jit(solution)/shard_map/ppermute | solution.py:26
  41.8 1.3 copy-start
  45.4 1.9 copy-start.1
  47.3 1.3 copy-start
  50.9 1.9 copy-start.1
  53.1 6.6 %copy-start.6 = (f32[256,256]{0,1:T(8,128)S(1)}, f32[256,256]{0,1:T(8,128)}, u32[]{:S(2)}) copy-start(f32[256,256]{0,1:T(8,128)} %copy.64) | copy-start | bytes 786436
  53.1 6.6 %copy-start.7 = (f32[256,256]{0,1:T(8,128)S(1)}, f32[256,256]{0,1:T(8,128)}, u32[]{:S(2)}) copy-start(f32[256,256]{0,1:T(8,128)} %copy.71) | copy-start | bytes 786436
  53.1 6.6 %copy-start.8 = (f32[2,2,2,256,256]{3,4,0,2,1:T(8,128)S(1)}, f32[2,2,2,256,256]{3,4,0,2,1:T(8,128)}, u32[]{:S(2)}) copy-start(f32[2,2,2,256,256]{3,4,0,2,1:T(8,128)} %get-tuple-element.57) | copy-start | bytes 6291460
  95.9 5.5 %copy-start.4 = (f32[1,1,2,256,256]{3,4,2,1,0:T(8,128)S(1)}, f32[1,1,2,256,256]{3,4,2,1,0:T(8,128)}, u32[]{:S(2)}) copy-start(f32[1,1,2,256,256]{3,4,2,1,0:T(8,128)} %copy.98) | copy-start | bytes 1572868
  148.6 1.3 copy-start.5
  180.4 5.0 %copy-start.13 = (f32[256,256]{0,1:T(8,128)S(1)}, f32[256,256]{0,1:T(8,128)}, u32[]{:S(2)}) copy-start(f32[256,256]{0,1:T(8,128)} %get-tuple-element.66) | copy-start | bytes 786436
  180.4 5.0 %copy-start.14 = (f32[256,256]{0,1:T(8,128)S(1)}, f32[256,256]{0,1:T(8,128)}, u32[]{:S(2)}) copy-start(f32[256,256]{0,1:T(8,128)} %get-tuple-element.67) | copy-start | bytes 786436
  180.4 11.1 %collective-permute-start.4 = (f32[2,2,32,320]{3,2,1,0:T(8,128)S(1)}, f32[2,2,32,320]{3,2,1,0:T(8,128)}, u32[]{:S(2)}, u32[]{:S(2)}) collective-permute-start(f32[2,2,32,320]{3,2,1,0:T(8,128)S(1)} %copy.124), channel_id=1, source_target_pairs={{16,0},{17,1},{18,2},{19,3},{20,4},{21,5},{22,6},{23,7},{24,8},{25... | collective-permute-start | bytes 491528 | tf_op jit(solution)/shard_map/ppermute | solution.py:13
  187.1 9.4 %collective-permute-start.5 = (f32[2,2,32,320]{3,2,1,0:T(8,128)}, f32[2,2,32,320]{3,2,1,0:T(8,128)}, u32[]{:S(2)}, u32[]{:S(2)}) collective-permute-start(f32[2,2,32,320]{3,2,1,0:T(8,128)} %copy.126), channel_id=1, source_target_pairs={{0,16},{1,17},{2,18},{3,19},{4,20},{5,21},{6,22},{7,23},{8,24},{9,... | collective-permute-start | bytes 491528 | tf_op jit(solution)/shard_map/ppermute | solution.py:13
  198.8 118.5 %copy-start.11 = (f32[2,256,256]{1,2,0:T(8,128)S(1)}, f32[2,256,256]{1,2,0:T(8,128)}, u32[]{:S(2)}) copy-start(f32[2,256,256]{1,2,0:T(8,128)} %copy.129) | copy-start | bytes 1572868
  205.5 113.0 %collective-permute-start.6 = (f32[2,2,32,256]{3,2,1,0:T(8,128)}, f32[2,2,32,256]{3,2,1,0:T(8,128)S(1)}, u32[]{:S(2)}, u32[]{:S(2)}) collective-permute-start(f32[2,2,32,256]{3,2,1,0:T(8,128)} %get-tuple-element.91), channel_id=1, source_target_pairs={{1,0},{2,1},{3,2},{4,3},{5,4},{6,5},{7,6},{8,7},{9,8},{10,9},{11,1... | collective-permute-start | bytes 393224 | tf_op jit(solution)/shard_map/ppermute | solution.py:13
  206.8 154.7 %copy-start.3 = (f32[2,2,256,256]{2,3,1,0:T(8,128)S(1)}, f32[2,2,256,256]{2,3,1,0:T(8,128)}, u32[]{:S(2)}) copy-start(f32[2,2,256,256]{2,3,1,0:T(8,128)} %copy-done.2) | copy-start | bytes 3145732
  206.8 112.6 %collective-permute-start.7 = (f32[2,2,32,256]{3,2,1,0:T(8,128)S(1)}, f32[2,2,32,256]{3,2,1,0:T(8,128)S(1)}, u32[]{:S(2)}, u32[]{:S(2)}) collective-permute-start(f32[2,2,32,256]{3,2,1,0:T(8,128)S(1)} %get-tuple-element.90), channel_id=1, source_target_pairs={{0,1},{1,2},{2,3},{3,4},{4,5},{5,6},{6,7},{7,8},{8,9},{9,10},{10,1... | collective-permute-start | bytes 393224 | tf_op jit(solution)/shard_map/ppermute | solution.py:13
Sparse Core Ops, SparseCore 0:
  186.3 130.9 all-reduce.1
where the time goes:
time: 377 us; the launch traced here: 372 us
  waiting for transfers between devices  116 us (31%)
  matrix products  94.9 us (25%)
  local copies, waits for them, and re-layouts  67.2 us (18%)
  blocking collectives  39.5 us (10%)
  starting transfers between devices  21 us (6%)
  between operations  20.6 us (5%)
  other arithmetic  12.9 us (3%)
    psum x1, waiting for transfers between devices, local(): probe_total = lax.psum(probe_grad, ('row', 'col'))  106 us
    pmax x1, blocking collectives, local(): largest = lax.pmax(local_peak, ('row', 'col'))  39.5 us
    dynamic_update_slice x2, local copies, waits for them, and re-layouts, tile_gradient(): lax.dynamic_update_slice(gradient, current + pieces[position], start_at)  27.5 us
    dot_general x6, matrix products, transform(): ic = jnp.einsum('byx,xk->byk', imag_part, cosine, precision=high)  13.1 us
    dot_general x6, matrix products, transform(): rc = jnp.einsum('byx,xk->byk', real_part, cosine, precision=high)  12.6 us
    dot_general x6, matrix products, transform(): jnp.einsum('ky,byx->bkx', sine_tab, mid_im, precision=high)  12.4 us
    dot_general x6, matrix products, transform(): rs = jnp.einsum('byx,xk->byk', real_part, sine_tab, precision=high)  11.8 us
    ppermute x4, starting transfers between devices, passed_along(): lax.ppermute(value, axis, [(source, source + steps) for source in range(i...  11.8 us
  transfers between devices with their start and end apart: 9, of which 3 were waited for; matrix products, arithmetic and copies ran while one was open for 7% of the time, Pallas kernels for 0%

commit v1 on v0

--- a/solution.py
+++ b/solution.py
@@ -151,7 +151,7 @@
     current = object_in
     window = extended(current, (("row", 2), ("col", 3)), RIM)
     gradient, probe_grad = tile_gradient(window, probe_in, offsets, measured, constants)
-    probe_total = lax.psum(probe_grad, ("row", "col"))
+    probe_total = jnp.sum(lax.all_gather(probe_grad, ("row", "col")), axis=0)
     probe_next = probe_in - probe_rate * probe_total
     descent = rows_then_cols(gradient)
     local_peak = jnp.max(descent[:, 0] ** 2 + descent[:, 1] ** 2)

time: 377 us -> 289 us (0.77)
  waiting for transfers between devices: 116 us -> 15.3 us
  blocking collectives: 39.5 us -> 46.8 us
  other arithmetic: 12.9 us -> 18.7 us
  local copies, waits for them, and re-layouts: 67.2 us -> 63.2 us
    psum x1 -> x0, waiting for transfers between devices: 106 us -> none  [local(): probe_total = lax.psum(probe_grad, ('row', 'col'))]
    ppermute x4, waiting for transfers between devices: 0.01 us -> 7.55 us  [passed_along(): lax.ppermute(value, axis, [(source, source + steps) for source in range(i...]
    pmax x1, blocking collectives: 39.5 us -> 46.8 us  [local(): largest = lax.pmax(local_peak, ('row', 'col'))]
    reduce_sum x0 -> x1, other arithmetic: none -> 6.95 us  [local(): probe_total = jnp.sum(lax.all_gather(probe_grad, ('row', 'col')), axis=0)]
    unnamed x33 -> x27, local copies, waits for them, and re-layouts: 9.49 us -> 5.24 us
  transfers between devices with their start and end apart: 9 -> 9, of which waited for: 3 -> 4; matrix products, arithmetic and copies ran while one was open for 7% -> 20% of each run, Pallas kernels for 0% -> 0%
where the time goes in v1:
time: 289 us; the launch traced here: 284 us
  matrix products  95 us (33%)
  local copies, waits for them, and re-layouts  63.2 us (22%)
  blocking collectives  46.8 us (16%)
  starting transfers between devices  23.5 us (8%)
  between operations  20.8 us (7%)
  other arithmetic  18.7 us (6%)
  waiting for transfers between devices  15.3 us (5%)
    pmax x1, blocking collectives, local(): largest = lax.pmax(local_peak, ('row', 'col'))  46.8 us
    dynamic_update_slice x2, local copies, waits for them, and re-layouts, tile_gradient(): lax.dynamic_update_slice(gradient, current + pieces[position], start_at)  27.5 us
    dot_general x6, matrix products, transform(): rc = jnp.einsum('byx,xk->byk', real_part, cosine, precision=high)  13.1 us
    dot_general x6, matrix products, transform(): jnp.einsum('ky,byx->bkx', sine_tab, mid_im, precision=high)  12.9 us
    dot_general x6, matrix products, transform(): ic = jnp.einsum('byx,xk->byk', imag_part, cosine, precision=high)  12.6 us
    ppermute x4, starting transfers between devices, passed_along(): lax.ppermute(value, axis, [(source, source + steps) for source in range(i...  12.2 us
    dot_general x6, matrix products, transform(): isn = jnp.einsum('byx,xk->byk', imag_part, sine_tab, precision=high)  11.9 us
    dot_general x6, matrix products, transform(): rs = jnp.einsum('byx,xk->byk', real_part, sine_tab, precision=high)  11.5 us
  transfers between devices with their start and end apart: 9, of which 4 were waited for; matrix products, arithmetic and copies ran while one was open for 20% of the time, Pallas kernels for 0%

profile of v1, /device:TPU:0, one launch (start us, length us, event | category | flops | bytes accessed | tf_op | source)
XLA Modules:
  0.0 283.7 jit_solution(6781548442091855451)
XLA Ops:
  11.5 3.1 %collective-permute-start = (f32[2,2,32,256]{2,3,1,0:T(8,128)}, f32[2,2,32,256]{2,3,1,0:T(8,128)S(1)}, u32[]{:S(2)}, u32[]{:S(2)}) collective-permute-start(f32[2,2,32,256]{2,3,1,0:T(8,128)} %get-tuple-element.96), channel_id=1, source_target_pairs={{0,16},{1,17},{2,18},{3,19},{4,20},{5,21},{6,22},{7,23},{8,24},{9,... | collective-permute-start | bytes 393224 | tf_op jit(solution)/shard_map/ppermute | solution.py:24
  17.4 2.0 copy.98
  21.1 5.5 %collective-permute-start.2 = (f32[2,2,320,32]{2,3,1,0:T(8,128)S(1)}, f32[2,2,320,32]{2,3,1,0:T(8,128)S(1)}, u32[]{:S(2)}, u32[]{:S(2)}) collective-permute-start(f32[2,2,320,32]{2,3,1,0:T(8,128)S(1)} %get-tuple-element.84), channel_id=1, source_target_pairs={{0,1},{1,2},{2,3},{3,4},{4,5},{5,6},{6,7},{7,8},{8,9},{9,10},{10,1... | collective-permute-start | bytes 491528 | tf_op jit(solution)/shard_map/ppermute | solution.py:24
  26.7 2.4 collective-permute-done.3
  29.1 5.3 %collective-permute-done.2 = f32[2,2,320,32]{2,3,1,0:T(8,128)S(1)} collective-permute-done((f32[2,2,320,32]{2,3,1,0:T(8,128)S(1)}, f32[2,2,320,32]{2,3,1,0:T(8,128)S(1)}, u32[]{:S(2)}, u32[]{:S(2)}) %collective-permute-start.2) | collective-permute-done | bytes 163872 | tf_op jit(solution)/shard_map/ppermute | solution.py:24
  36.2 11.3 %while.5 = (s32[]{:T(128)}, f32[2,2,320,320]{2,3,1,0:T(8,128)S(1)}, s32[2,4]{1,0:T(2,128)S(1)}, f32[2,2,2,256,256]{3,4,0,2,1:T(8,128)}, s32[]{:T(128)}) while((s32[]{:T(128)}, f32[2,2,320,320]{2,3,1,0:T(8,128)S(1)}, s32[2,4]{1,0:T(2,128)S(1)}, f32[2,2,2,256,256]{3,4,0,2,1:T(8,128)}, s32[]{:T(128)}) %tuple.63), condition=%wide.while_cond.4, body=%wide.while_body.4.sunk | while | flops 2 | bytes 21495996 | solution.py:91
  47.6 3.4 %fusion.116 = f32[2,256,256]{2,1,0:T(8,128)S(1)} fusion(f32[2,2,2,256,256]{3,4,0,2,1:T(8,128)} %get-tuple-element.57, f32[256,256]{0,1:T(8,128)} %copy.71, f32[256,256]{0,1:T(8,128)} %copy.64), kind=kOutput, calls=%fused_computation.184 | convolution fusion | flops 404029440 | bytes 2097152 | tf_op jit(solution)/shard_map/byx,xk->byk/dot_general | solution.py:54
  50.9 3.2 %fusion.112 = f32[2,256,256]{2,1,0:T(8,128)S(1)} fusion(f32[2,2,2,256,256]{3,4,0,2,1:T(8,128)} %get-tuple-element.57, f32[256,256]{0,1:T(8,128)} %copy.71, f32[256,256]{0,1:T(8,128)} %copy.64), kind=kOutput, calls=%fused_computation.180 | convolution fusion | flops 404029440 | bytes 2097152 | tf_op jit(solution)/shard_map/byx,xk->byk/dot_general | solution.py:56
  61.6 2.3 fusion.23
  73.3 2.1 fusion.21
  84.5 2.1 convolution_subtract_fusion.3
  97.7 2.3 fusion.92
  100.0 1.9 fusion.12
  103.8 1.9 fusion.13
  109.5 2.2 add_bitcast_fusion
  120.9 2.1 fusion.78
  134.1 2.3 fusion.5
  140.1 2.9 %fusion.38 = (f32[256,256]{0,1:T(8,128)S(1)}, f32[256,256]{0,1:T(8,128)S(1)}, f32[2,1,256,256]{2,3,0,1:T(8,128)S(1)}, f32[2,1,256,256]{2,3,0,1:T(8,128)}) fusion(f32[2,256,256]{1,2,0:T(8,128)S(1)} %fusion.1, f32[2,2,2,256,256]{3,4,0,2,1:T(8,128)S(1)} %copy-done.8, f32[256,256]{0,1:T(8,128)S(1)} %copy-done.6, f32[256,256]{0,1:T(8,128)S(1)} %copy-done.7, ...), kind=kOutput, calls=%fused_computation.86 | convolution fusion | flops 405602304 | bytes 4718592 | tf_op jit(solution)/shard_map/ky,byx->bkx/dot_general | solution.py:60
  152.5 13.5 %dynamic_update_slice.6 = f32[2,2,320,320]{2,3,1,0:T(8,128)S(1)} dynamic-update-slice(f32[2,2,320,320]{2,3,1,0:T(8,128)S(1)} %broadcast_in_dim.2, f32[2,2,256,256]{2,3,1,0:T(8,128)} %fusion.25, s32[]{:T(128)} %constant.162.clone.1, s32[]{:T(128)} %constant.162.clone.1, s32[]{:T(128)S(6)} %select_n.155, s32[]{:T(128)S(6)} %select_n.156) | dynamic-update-slice | bytes 2097156 | tf_op jit(solution)/shard_map/dynamic_update_slice | solution.py:120
  165.9 2.4 fusion.27
  168.3 14.0 %dynamic_update_slice.7 = f32[2,2,320,320]{2,3,1,0:T(8,128)S(1)} dynamic-update-slice(f32[2,2,320,320]{2,3,1,0:T(8,128)S(1)} %dynamic_update_slice.6, f32[2,2,256,256]{2,3,1,0:T(8,128)} %fusion.27, s32[]{:T(128)} %constant.162.clone.1, s32[]{:T(128)} %constant.162.clone.1, s32[]{:T(128)S(6)} %select_n.157, s32[]{:T(128)S(6)} %select_n.158) | dynamic-update-slice | bytes 2097156 | tf_op jit(solution)/shard_map/dynamic_update_slice | solution.py:120
  186.1 2.0 copy.126
  188.1 4.4 %collective-permute-start.5 = (f32[2,2,32,320]{3,2,1,0:T(8,128)}, f32[2,2,32,320]{3,2,1,0:T(8,128)}, u32[]{:S(2)}, u32[]{:S(2)}) collective-permute-start(f32[2,2,32,320]{3,2,1,0:T(8,128)} %copy.126), channel_id=1, source_target_pairs={{0,16},{1,17},{2,18},{3,19},{4,20},{5,21},{6,22},{7,23},{8,24},{9,... | collective-permute-start | bytes 491528 | tf_op jit(solution)/shard_map/ppermute | solution.py:13
  192.5 2.0 copy.125
  194.5 2.0 slice_add_fusion.1
  196.6 4.3 %scatter-add.14 = f32[2,2,256,320]{2,3,1,0:T(8,128)S(1)} dynamic-update-slice(f32[2,2,256,320]{2,3,1,0:T(8,128)S(1)} %slice.249, f32[2,2,32,320]{2,3,1,0:T(8,128)} %slice_add_fusion.1, s32[]{:T(128)} %constant.162.clone.1, s32[]{:T(128)} %constant.162.clone.1, s32[]{:T(128)} %constant.175.clone.1, s32[]{:T(128)} %constant.162.clone.1) | dynamic-update-slice | bytes 327684 | tf_op jit(solution)/shard_map/scatter-add | solution.py:134
  202.1 2.7 scatter-add.15
  206.4 5.1 %collective-permute-start.7 = (f32[2,2,32,256]{3,2,1,0:T(8,128)S(1)}, f32[2,2,32,256]{3,2,1,0:T(8,128)S(1)}, u32[]{:S(2)}, u32[]{:S(2)}) collective-permute-start(f32[2,2,32,256]{3,2,1,0:T(8,128)S(1)} %get-tuple-element.90), channel_id=1, source_target_pairs={{0,1},{1,2},{2,3},{3,4},{4,5},{5,6},{6,7},{7,8},{8,9},{9,10},{10,1... | collective-permute-start | bytes 393224 | tf_op jit(solution)/shard_map/ppermute | solution.py:13
  211.5 5.1 %collective-permute-done.6 = f32[2,2,32,256]{3,2,1,0:T(8,128)S(1)} collective-permute-done((f32[2,2,32,256]{3,2,1,0:T(8,128)S(1)}, f32[2,2,32,256]{3,2,1,0:T(8,128)S(1)}, u32[]{:S(2)}, u32[]{:S(2)}) %collective-permute-start.6) | collective-permute-done | bytes 131104 | tf_op jit(solution)/shard_map/ppermute | solution.py:13
  216.7 2.4 collective-permute-done.7
  219.9 46.8 %pmax.7 = f32[]{:T(128)} all-reduce(f32[]{:T(128)} %fusion.29), channel_id=1, replica_groups=mesh['row'=2,'col'=16] {'row','col'}, use_global_device_ids=true, to_apply=%region_1.2 | all-reduce | flops 1 | bytes 8 | tf_op jit(solution)/shard_map/pmax | solution.py:158
  268.9 6.9 %reduce_sum.29 = f32[2,256,256]{2,1,0:T(8,128)S(1)} reduce(f32[32,2,256,256]{3,2,1,0:T(8,128)} %bitcast.294, f32[]{:T(128)} %constant.160.clone.1), dimensions={0}, to_apply=%region_4.5 | reduce | flops 4063232 | bytes 17301508 | tf_op jit(solution)/shard_map/reduce_sum | solution.py:154
  (124 shorter events, 101.7 us)
Async XLA Ops:
  7.2 7.5 %copy-start.11 = (f32[2,256,256]{2,1,0:T(8,128)S(1)}, f32[2,256,256]{2,1,0:T(8,128)}, u32[]{:S(2)}) copy-start(f32[2,256,256]{2,1,0:T(8,128)} %param.13) | copy-start | bytes 1572868
  7.2 261.7 %all-gather.3.cloned.1.call-start = ((), (), s32[]{:S(2)}) async-start(), calls=%async_computation | async-start | bytes 17301504 | tf_op jit(solution)/shard_map/all_gather | solution.py:154
  8.8 25.6 %copy-start.2 = (f32[2,2,256,256]{2,3,1,0:T(8,128)}, f32[2,2,256,256]{2,3,1,0:T(8,128)S(1)}, u32[]{:S(2)}) copy-start(f32[2,2,256,256]{2,3,1,0:T(8,128)S(1)} %copy.128) | copy-start | bytes 3145732
  10.1 9.4 %copy-start.13 = (s32[1,1,2,2]{3,2,1,0:T(2,128)S(1)}, s32[1,1,2,2]{3,2,1,0:T(2,128)}, u32[]{:S(2)}) copy-start(s32[1,1,2,2]{3,2,1,0:T(2,128)} %param.14) | copy-start | bytes 52
  10.1 9.5 %collective-permute-start.1 = (f32[2,2,32,256]{2,3,1,0:T(8,128)}, f32[2,2,32,256]{2,3,1,0:T(8,128)S(1)}, u32[]{:S(2)}, u32[]{:S(2)}) collective-permute-start(f32[2,2,32,256]{2,3,1,0:T(8,128)} %get-tuple-element.97), channel_id=1, source_target_pairs={{16,0},{17,1},{18,2},{19,3},{20,4},{21,5},{22,6},{23,7},{24,8},{25... | collective-permute-start | bytes 393224 | tf_op jit(solution)/shard_map/ppermute | solution.py:26
  11.5 8.0 %collective-permute-start = (f32[2,2,32,256]{2,3,1,0:T(8,128)}, f32[2,2,32,256]{2,3,1,0:T(8,128)S(1)}, u32[]{:S(2)}, u32[]{:S(2)}) collective-permute-start(f32[2,2,32,256]{2,3,1,0:T(8,128)} %get-tuple-element.96), channel_id=1, source_target_pairs={{0,16},{1,17},{2,18},{3,19},{4,20},{5,21},{6,22},{7,23},{8,24},{9,... | collective-permute-start | bytes 393224 | tf_op jit(solution)/shard_map/ppermute | solution.py:24
  19.5 9.5 %copy-start.9 = (f32[2,2,32,256]{2,3,1,0:T(8,128)}, f32[2,2,32,256]{2,3,1,0:T(8,128)S(1)}, u32[]{:S(2)}) copy-start(f32[2,2,32,256]{2,3,1,0:T(8,128)S(1)} %collective-permute-done.1) | copy-start | bytes 393220
  19.6 9.5 %copy-start.10 = (f32[2,2,32,256]{2,3,1,0:T(8,128)}, f32[2,2,32,256]{2,3,1,0:T(8,128)S(1)}, u32[]{:S(2)}) copy-start(f32[2,2,32,256]{2,3,1,0:T(8,128)S(1)} %collective-permute-done) | copy-start | bytes 393220
  19.8 9.3 %collective-permute-start.3 = (f32[2,2,320,32]{2,3,1,0:T(8,128)S(1)}, f32[2,2,320,32]{2,3,1,0:T(8,128)S(1)}, u32[]{:S(2)}, u32[]{:S(2)}) collective-permute-start(f32[2,2,320,32]{2,3,1,0:T(8,128)S(1)} %get-tuple-element.85), channel_id=1, source_target_pairs={{1,0},{2,1},{3,2},{4,3},{5,4},{6,5},{7,6},{8,7},{9,8},{10,9},{11,1... | collective-permute-start | bytes 491528 | tf_op jit(solution)/shard_map/ppermute | solution.py:26
  21.1 13.3 %collective-permute-start.2 = (f32[2,2,320,32]{2,3,1,0:T(8,128)S(1)}, f32[2,2,320,32]{2,3,1,0:T(8,128)S(1)}, u32[]{:S(2)}, u32[]{:S(2)}) collective-permute-start(f32[2,2,320,32]{2,3,1,0:T(8,128)S(1)} %get-tuple-element.84), channel_id=1, source_target_pairs={{0,1},{1,2},{2,3},{3,4},{4,5},{5,6},{6,7},{7,8},{8,9},{9,10},{10,1... | collective-permute-start | bytes 491528 | tf_op jit(solution)/shard_map/ppermute | solution.py:24
  36.2 1.3 copy-start
  39.8 1.9 copy-start.1
  41.7 1.3 copy-start
  45.3 1.9 copy-start.1
  47.5 6.6 %copy-start.6 = (f32[256,256]{0,1:T(8,128)S(1)}, f32[256,256]{0,1:T(8,128)}, u32[]{:S(2)}) copy-start(f32[256,256]{0,1:T(8,128)} %copy.71) | copy-start | bytes 786436
  47.6 6.6 %copy-start.7 = (f32[256,256]{0,1:T(8,128)S(1)}, f32[256,256]{0,1:T(8,128)}, u32[]{:S(2)}) copy-start(f32[256,256]{0,1:T(8,128)} %copy.64) | copy-start | bytes 786436
  47.6 6.6 %copy-start.8 = (f32[2,2,2,256,256]{3,4,0,2,1:T(8,128)S(1)}, f32[2,2,2,256,256]{3,4,0,2,1:T(8,128)}, u32[]{:S(2)}) copy-start(f32[2,2,2,256,256]{3,4,0,2,1:T(8,128)} %get-tuple-element.57) | copy-start | bytes 6291460
  90.3 5.5 %copy-start.4 = (f32[1,1,2,256,256]{3,4,2,1,0:T(8,128)S(1)}, f32[1,1,2,256,256]{3,4,2,1,0:T(8,128)}, u32[]{:S(2)}) copy-start(f32[1,1,2,256,256]{3,4,2,1,0:T(8,128)} %copy.98) | copy-start | bytes 1572868
  151.0 1.3 copy-start.5
  184.4 8.1 %collective-permute-start.4 = (f32[2,2,32,320]{3,2,1,0:T(8,128)}, f32[2,2,32,320]{3,2,1,0:T(8,128)}, u32[]{:S(2)}, u32[]{:S(2)}) collective-permute-start(f32[2,2,32,320]{3,2,1,0:T(8,128)} %copy.124), channel_id=1, source_target_pairs={{16,0},{17,1},{18,2},{19,3},{20,4},{21,5},{22,6},{23,7},{24,8},{25... | collective-permute-start | bytes 491528 | tf_op jit(solution)/shard_map/ppermute | solution.py:13
  188.1 12.8 %collective-permute-start.5 = (f32[2,2,32,320]{3,2,1,0:T(8,128)}, f32[2,2,32,320]{3,2,1,0:T(8,128)}, u32[]{:S(2)}, u32[]{:S(2)}) collective-permute-start(f32[2,2,32,320]{3,2,1,0:T(8,128)} %copy.126), channel_id=1, source_target_pairs={{0,16},{1,17},{2,18},{3,19},{4,20},{5,21},{6,22},{7,23},{8,24},{9,... | collective-permute-start | bytes 491528 | tf_op jit(solution)/shard_map/ppermute | solution.py:13
  204.9 62.5 %copy-start.3 = (f32[2,2,256,256]{2,3,1,0:T(8,128)S(1)}, f32[2,2,256,256]{2,3,1,0:T(8,128)}, u32[]{:S(2)}) copy-start(f32[2,2,256,256]{2,3,1,0:T(8,128)} %copy-done.2) | copy-start | bytes 3145732
  204.9 11.8 %collective-permute-start.6 = (f32[2,2,32,256]{3,2,1,0:T(8,128)S(1)}, f32[2,2,32,256]{3,2,1,0:T(8,128)S(1)}, u32[]{:S(2)}, u32[]{:S(2)}) collective-permute-start(f32[2,2,32,256]{3,2,1,0:T(8,128)S(1)} %get-tuple-element.91), channel_id=1, source_target_pairs={{1,0},{2,1},{3,2},{4,3},{5,4},{6,5},{7,6},{8,7},{9,8},{10,9},{11,1... | collective-permute-start | bytes 393224 | tf_op jit(solution)/shard_map/ppermute | solution.py:13
  206.4 12.7 %collective-permute-start.7 = (f32[2,2,32,256]{3,2,1,0:T(8,128)S(1)}, f32[2,2,32,256]{3,2,1,0:T(8,128)S(1)}, u32[]{:S(2)}, u32[]{:S(2)}) collective-permute-start(f32[2,2,32,256]{3,2,1,0:T(8,128)S(1)} %get-tuple-element.90), channel_id=1, source_target_pairs={{0,1},{1,2},{2,3},{3,4},{4,5},{5,6},{6,7},{7,8},{8,9},{9,10},{10,1... | collective-permute-start | bytes 393224 | tf_op jit(solution)/shard_map/ppermute | solution.py:13
  268.9 7.0 %copy-start.12 = (f32[2,256,256]{2,1,0:T(8,128)S(1)}, f32[2,256,256]{2,1,0:T(8,128)}, u32[]{:S(2)}) copy-start(f32[2,256,256]{2,1,0:T(8,128)} %param.13) | copy-start | bytes 1572868
Sparse Core Ops, SparseCore 0:
  144.2 121.6 all-gather.2
